TPU v7x, 32 devices: a whole 2x2x4 slice. The times are simulated.
32 devices in a mesh: freq: 4 (over y, core), stn: 8 (over z, x).
Axes of the slice: x: 2, y: 2, z: 4, core: 2. Of those that a mesh axis runs over, the one named last changes fastest.
Arguments:
- samples: bfloat16 [4, 256, 24, 2, 128], P('freq', 'stn'), may hold values from -8 to 8, as said below
- window: float32 [128], replicated, may hold values from 0.1 to 1
- group_of_device: int32 [8], replicated, may hold values from 0 to 7, each once
- owner_map: int32 [8, 8], replicated, may hold values from 0 to 7, as said below
Outputs:
- owned: bfloat16 [2, 32, 8, 8, 1024], P(None, None, 'stn', 'freq')
Inputs may be any that keep to these rules, and one draw needn't show every extreme that they name: `samples`: samples are finite and bounded. Every row and every column of owner_map names each stn index exactly once.
All inputs are finite; a program needn't handle non-finite values.
Results may differ from a plain program's by a relative error of at most 0.0065.
Values may be sent and summed in bfloat16 or wider, within the bound.
No kernel may reach another device: no remote copies, remote signals or barrier semaphores. Data moves between devices by JAX's collectives and lax.ppermute only.
A program may use at most 64 MiB of HBM per device.

v0:
```python
import math

import jax
import jax.numpy as jnp
from jax import lax
from jax.sharding import PartitionSpec as P

FFT_LEN = 128
AVG = 16
SPEC = 24
CH_OUT = 8


def channel_matrix(window):
    length = window.shape[0]
    index = jnp.arange(length, dtype=jnp.int32)
    product = index[:, None] * index[None, :] % length
    theta = product.astype(jnp.float32) * (2.0 * math.pi / length)
    weights = window[:, None] / math.sqrt(length)
    cosine = weights * jnp.cos(theta)
    sine = weights * jnp.sin(theta)
    upper = jnp.concatenate([cosine, -sine], axis=1)
    lower = jnp.concatenate([sine, cosine], axis=1)
    return jnp.concatenate([upper, lower], axis=0)


def split_matrix(matrix):
    high = matrix.astype(jnp.bfloat16)
    low = (matrix - high.astype(jnp.float32)).astype(jnp.bfloat16)
    return (high, low)


def channelize(block, high, low):
    rows = block.shape[0]
    flat = block.reshape(rows * SPEC, 2 * FFT_LEN)
    spectra = jnp.dot(flat, high, preferred_element_type=jnp.float32) + jnp.dot(
        flat, low, preferred_element_type=jnp.float32
    )
    spectra = spectra.astype(jnp.bfloat16).reshape(rows, SPEC, 2, CH_OUT, AVG)
    return spectra.transpose(3, 0, 2, 1, 4).reshape(CH_OUT, rows, 2 * SPEC * AVG)


def with_swapped(spectra):
    half = spectra.shape[2] // 2
    return jnp.stack(
        [spectra, jnp.concatenate([spectra[..., half:], -spectra[..., :half]], axis=-1)]
    )


def correlate(stacked, remote):
    block = jnp.einsum("pcak,cbk->pcab", stacked, remote, preferred_element_type=jnp.float32)
    return (block * (1.0 / (AVG * SPEC))).astype(jnp.bfloat16)


def channel_plan(local, group_of_device, owner_map, device_of_group, here, groups):
    rows_in = local.shape[1]
    spread = groups // CH_OUT
    quarter = here % spread
    copies = jnp.repeat(local, spread, axis=0)
    turned = lax.all_to_all(copies, "stn", split_axis=0, concat_axis=1, tiled=True)
    span = CH_OUT * rows_in
    mine = lax.dynamic_slice_in_dim(turned, quarter * span, span, 1)
    block = correlate(with_swapped(mine), turned)
    order = jnp.arange(groups, dtype=jnp.int32)
    column_for = (
        jnp.zeros((groups, groups), jnp.int32)
        .at[order[:, None], owner_map]
        .set(jnp.broadcast_to(order[None, :], (groups, groups)))
    )
    row_source = quarter * CH_OUT + jnp.arange(CH_OUT, dtype=jnp.int32)
    row_group = group_of_device[row_source]
    column_device = device_of_group[column_for[row_group]]
    vis = block.reshape(2, CH_OUT, rows_in, groups, rows_in).transpose(0, 1, 3, 2, 4)
    picked = jnp.take_along_axis(vis, column_device[None, :, :, None, None], axis=2)
    outgoing = picked.reshape(2, CH_OUT, groups, rows_in * rows_in)
    received = lax.all_to_all(outgoing, "stn", split_axis=2, concat_axis=2, tiled=True)
    arranged = received.reshape(2, CH_OUT, CH_OUT, spread, rows_in * rows_in).transpose(
        0, 2, 3, 1, 4
    )
    arranged = arranged.reshape(2, CH_OUT, groups, rows_in * rows_in)
    return jnp.take(arranged, device_of_group, axis=2)


def shards(samples, window, group_of_device, owner_map):
    groups = lax.axis_size("stn")
    here = lax.axis_index("stn")
    high, low = split_matrix(channel_matrix(window))
    local = channelize(samples[0], high, low)
    order = jnp.arange(groups, dtype=jnp.int32)
    device_of_group = jnp.zeros((groups,), jnp.int32).at[group_of_device].set(order)
    by_group = channel_plan(local, group_of_device, owner_map, device_of_group, here, groups)
    regrouped = lax.all_to_all(by_group, "freq", split_axis=2, concat_axis=1, tiled=True)
    return regrouped[:, :, None]


def solution(mesh):
    return jax.shard_map(
        shards,
        mesh=mesh,
        in_specs=(P("freq", "stn", None, None, None), P(), P(), P()),
        out_specs=P(None, None, "stn", "freq", None),
        check_vma=False,
    )
```

profile of v0, /device:TPU:0, one launch (start us, length us, event | category | flops | bytes accessed | tf_op | source)
XLA Modules:
  0.0 58.0 jit_solution(11295048349949106297)
XLA Ops:
  0.0 0.7 %broadcast_multiply_fusion = f32[128]{0:T(128)S(1)} fusion(f32[128]{0:T(128)} %param.5), kind=kLoop, calls=%fused_computation.69 | loop fusion | flops 128 | bytes 1024 | tf_op jit(solution)/shard_map/div | solution.py:19
  1.0 1.3 %fusion.7 = f32[256,768]{1,0:T(8,128)S(1)} fusion(bf16[96,8,2,128]{3,2,1,0:T(2,128)(2,1)} %bitcast.75, f32[128,128]{1,0:T(8,128)S(1)} %get-tuple-element.9, f32[128,128]{1,0:T(8,128)S(1)} %get-tuple-element.8, f32[128,128]{1,0:T(8,128)S(1)} %get-tuple-element.7), kind=kOutput, calls=%fused_computation.18 | convolution fusion | flops 101187584 | bytes 1376256 | tf_op jit(solution)/shard_map/dot_general | solution.py:36
  2.3 0.3 fusion.2
  2.6 3.4 %reshape.92 = bf16[32,24,2,8,16]{1,0,4,3,2:T(8,128)(2,1)S(1)} reshape(bf16[768,256]{0,1:T(8,128)(2,1)S(1)} %fusion.2) | data formatting | bytes 786432 | tf_op jit(solution)/shard_map/reshape | solution.py:39
  6.1 2.9 %copy.28 = bf16[8,32,2,24,16]{1,4,3,2,0:T(8,128)(2,1)} copy(bf16[8,32,2,24,16]{3,1,4,0,2:T(8,128)(2,1)S(1)} %bitcast.70) | data formatting | bytes 786432 | tf_op jit(solution)/shard_map/transpose | solution.py:40
  8.9 2.3 %copy.29 = bf16[8,32,768]{2,1,0:T(8,128)(2,1)} copy(bf16[8,32,768]{1,2,0:T(8,128)(2,1)} %bitcast.71) | data formatting | bytes 786432 | tf_op jit(solution)/shard_map/reshape;broadcast_in_dim;reshape | solution.py:59
  11.3 7.3 %all-to-all-start = ((bf16[8,32,768]{2,1,0:T(8,128)(2,1)}), bf16[8,32,768]{2,1,0:T(8,128)(2,1)S(1)}, u32[]{:S(2)}, u32[]{:S(2)}) async-start(bf16[8,32,768]{2,1,0:T(8,128)(2,1)} %copy.29), calls=%async_computation | async-start | bytes 786432 | tf_op jit(solution)/shard_map/all_to_all | solution.py:60
  18.8 0.6 %gather_fusion = s32[8]{0:T(128)S(1)} fusion(s32[8]{0:T(128)S(1)} %copy-done, s32[1024]{0:T(1024)S(1)} %pad_clamp_fusion.3), kind=kCustom, calls=%fused_computation | custom fusion | bytes 96 | tf_op jit(solution)/shard_map/gather | solution.py:71
  19.5 3.5 %scatter_fusion = s32[8,8]{1,0:T(8,128)S(1)} fusion(s32[8,8]{1,0:T(8,128)S(1)} %broadcast.121, s32[64]{0:T(128)S(1)} %reshape.144, s32[64]{0:T(128)S(1)} %reshape.146), kind=kCustom, calls=%fused_computation.6 | custom fusion | bytes 1280 | tf_op jit(solution)/shard_map/scatter | solution.py:68
  22.9 0.6 gather_fusion.1
  23.6 0.6 %scatter_custom_fusion = s32[8]{0:T(128)S(1)} fusion(s32[8]{0:T(128)S(1)} %compare_select_fusion.6, s32[8]{0:T(128)S(1)} %iota.20, s32[]{:T(128)} %constant.43.clone.1), kind=kCustom, calls=%fused_computation.70 | custom fusion | bytes 36 | tf_op jit(solution)/shard_map/scatter | solution.py:90
  24.2 0.8 %gather_fusion.2 = s32[64]{0:T(128)S(1)} fusion(s32[8]{0:T(128)S(1)} %scatter_custom_fusion, s32[1024]{0:T(1024)S(1)} %pad_clamp_fusion.1), kind=kCustom, calls=%fused_computation.2 | custom fusion | bytes 768 | tf_op jit(solution)/shard_map/gather | solution.py:72
  25.3 5.0 %all-to-all-done = bf16[8,32,768]{2,1,0:T(8,128)(2,1)S(1)} async-done(((bf16[8,32,768]{2,1,0:T(8,128)(2,1)}), bf16[8,32,768]{2,1,0:T(8,128)(2,1)S(1)}, u32[]{:S(2)}, u32[]{:S(2)}) %all-to-all-start) | async-done | bytes 393248 | tf_op jit(solution)/shard_map/all_to_all | solution.py:60
  30.3 0.4 fusion.3
  30.7 0.4 reshape.95
  31.2 0.9 %copy.30 = bf16[2,8,32,8,32]{4,2,3,1,0:T(8,128)(2,1)S(1)} copy(bf16[2,8,32,8,32]{2,1,4,3,0:T(8,128)(2,1)S(1)} %reshape.95) | data formatting | bytes 524288 | tf_op jit(solution)/shard_map/reshape | solution.py:73
  32.1 0.8 %gather_fusion.4 = bf16[64,2,32,32]{3,2,1,0:T(8,128)(2,1)S(1)} fusion(bf16[2,8,8,32,32]{4,3,2,1,0:T(8,128)(2,1)S(1)} %bitcast.73, s32[64]{0:T(128)S(1)} %reshape.130), kind=kCustom, calls=%fused_computation.4 | custom fusion | bytes 524800 | tf_op jit(solution)/shard_map/jit(take_along_axis)/gather | solution.py:74
  33.0 1.2 %gather.32 = bf16[2,8,8,1024]{3,2,1,0:T(8,128)(2,1)S(1)} reshape(bf16[2,8,8,32,32]{4,3,2,1,0:T(8,128)(2,1)S(1)} %bitcast.72) | data formatting | bytes 524288 | tf_op jit(solution)/shard_map/jit(take_along_axis)/gather | solution.py:74
  34.2 0.9 %copy.32 = bf16[2,8,8,1024]{3,1,0,2:T(8,128)(2,1)} copy(bf16[2,8,8,1024]{3,2,1,0:T(8,128)(2,1)S(1)} %broadcast_select_fusion) | data formatting | bytes 524288 | tf_op jit(solution)/shard_map/jit(take_along_axis)/select_n | solution.py:74
  35.1 3.6 %all-to-all-start.1 = ((bf16[2,8,8,1024]{3,1,0,2:T(8,128)(2,1)}), bf16[2,8,8,1024]{3,1,0,2:T(8,128)(2,1)S(1)}, u32[]{:S(2)}, u32[]{:S(2)}) async-start(bf16[2,8,8,1024]{3,1,0,2:T(8,128)(2,1)} %copy.32), calls=%async_computation.1 | async-start | bytes 524288 | tf_op jit(solution)/shard_map/all_to_all | solution.py:76
  38.8 8.8 %all-to-all-done.1 = bf16[2,8,8,1024]{3,1,0,2:T(8,128)(2,1)S(1)} async-done(((bf16[2,8,8,1024]{3,1,0,2:T(8,128)(2,1)}), bf16[2,8,8,1024]{3,1,0,2:T(8,128)(2,1)S(1)}, u32[]{:S(2)}, u32[]{:S(2)}) %all-to-all-start.1) | async-done | bytes 262176 | tf_op jit(solution)/shard_map/all_to_all | solution.py:76
  47.7 0.6 gather_fusion.3
  48.4 8.6 %all_to_all.32 = bf16[2,8,8,1024]{3,1,0,2:T(8,128)(2,1)S(1)} all-to-all(bf16[2,8,8,1024]{3,1,0,2:T(8,128)(2,1)S(1)} %select_bitcast_fusion), channel_id=1, replica_groups=mesh['freq'=4,'stn'=8] {'freq'}, dimensions={2} | all-to-all | bytes 524288 | tf_op jit(solution)/shard_map/all_to_all | solution.py:92
  57.0 1.0 %copy.36 = bf16[2,32,1,2,1024]{4,3,2,1,0:T(2,128)(2,1)} copy(bf16[2,32,1,2,1024]{4,1,3,0,2:T(8,128)(2,1)S(1)} %bitcast.82) | data formatting | bytes 524288 | tf_op jit(solution)/shard_map/broadcast_in_dim | solution.py:93
  (36 shorter events, 1.4 us)
Async XLA Ops:
  0.0 2.3 %copy-start.1 = (bf16[1,32,24,2,128]{4,3,2,1,0:T(2,128)(2,1)S(1)}, bf16[1,32,24,2,128]{4,3,2,1,0:T(2,128)(2,1)}, u32[]{:S(2)}) copy-start(bf16[1,32,24,2,128]{4,3,2,1,0:T(2,128)(2,1)} %param.4) | copy-start | bytes 1179652
  8.9 9.6 %copy-start.2 = (s32[8,8]{1,0:T(8,128)S(1)}, s32[8,8]{1,0:T(8,128)}, u32[]{:S(2)}) copy-start(s32[8,8]{1,0:T(8,128)} %param.7) | copy-start | bytes 772
  8.9 9.8 %copy-start = (s32[8]{0:T(128)S(1)}, s32[8]{0:T(128)}, u32[]{:S(2)}) copy-start(s32[8]{0:T(128)} %param.6) | copy-start | bytes 100
  11.3 19.0 %all-to-all-start = ((bf16[8,32,768]{2,1,0:T(8,128)(2,1)}), bf16[8,32,768]{2,1,0:T(8,128)(2,1)S(1)}, u32[]{:S(2)}, u32[]{:S(2)}) async-start(bf16[8,32,768]{2,1,0:T(8,128)(2,1)} %copy.29), calls=%async_computation | async-start | bytes 786432 | tf_op jit(solution)/shard_map/all_to_all | solution.py:60
  35.1 12.5 %all-to-all-start.1 = ((bf16[2,8,8,1024]{3,1,0,2:T(8,128)(2,1)}), bf16[2,8,8,1024]{3,1,0,2:T(8,128)(2,1)S(1)}, u32[]{:S(2)}, u32[]{:S(2)}) async-start(bf16[2,8,8,1024]{3,1,0,2:T(8,128)(2,1)} %copy.32), calls=%async_computation.1 | async-start | bytes 524288 | tf_op jit(solution)/shard_map/all_to_all | solution.py:76
where the time goes:
time: 58.4 us; the launch traced here: 58 us
  local copies, waits for them, and re-layouts  21.1 us (36%)
  waiting for transfers between devices  13.8 us (24%)
  starting transfers between devices  10.9 us (19%)
  blocking collectives  8.59 us (15%)
  matrix products  2.02 us (3%)
  other arithmetic  1.33 us (2%)
    all_to_all x1, waiting for transfers between devices, channel_plan(): lax.all_to_all(outgoing, 'stn', split_axis=2, concat_axis=2, tiled=True)  8.8 us
    all_to_all x1, blocking collectives, shards(): lax.all_to_all(by_group, 'freq', split_axis=2, concat_axis=1, tiled=True)  8.59 us
    all_to_all x1, starting transfers between devices, channel_plan(): lax.all_to_all(copies, 'stn', split_axis=0, concat_axis=1, tiled=True)  7.28 us
    all_to_all x1, waiting for transfers between devices, channel_plan(): lax.all_to_all(copies, 'stn', split_axis=0, concat_axis=1, tiled=True)  5 us
    all_to_all x1, starting transfers between devices, channel_plan(): lax.all_to_all(outgoing, 'stn', split_axis=2, concat_axis=2, tiled=True)  3.64 us
    scatter x1, local copies, waits for them, and re-layouts, channel_plan(): column_for = jnp.zeros((groups, groups), jnp.int32).at[order[:, None], ow...  3.45 us
    reshape x1, local copies, waits for them, and re-layouts, channelize(): spectra = spectra.astype(jnp.bfloat16).reshape(rows, SPEC, 2, CH_OUT, AVG)  3.43 us
    transpose x1, local copies, waits for them, and re-layouts, channelize(): spectra.transpose(3, 0, 2, 1, 4).reshape(CH_OUT, rows, 2 * SPEC * AVG)  2.86 us
  transfers between devices with their start and end apart: 2, of which 2 were waited for; matrix products, arithmetic and copies ran while one was open for 11% of the time, Pallas kernels for 0%

commit v1 on v0

v1 whole, which is shorter than its diff:
```python
import functools
import math

import jax
import jax.numpy as jnp
import numpy as np
from jax import lax
from jax.experimental import pallas as pl
from jax.experimental.pallas import tpu as pltpu
from jax.sharding import PartitionSpec as P

FFT_LEN = 128
AVG = 16
SPEC = 24
CH_OUT = 8
LANES = 128


def trig_table():
    index = np.arange(FFT_LEN)
    theta = (index[:, None] * index[None, :] % FFT_LEN) * (2.0 * math.pi / FFT_LEN)
    table = np.concatenate([np.cos(theta), np.sin(theta)], axis=0) / math.sqrt(FFT_LEN)
    return table.astype(np.float32)


def barrel(values, lane_chunk):
    n = len(values)
    step = 1
    while step < n:
        bit = (lane_chunk // step) % 2 == 1
        values = [jnp.where(bit, values[(i - step) % n], values[i]) for i in range(n)]
        step *= 2
    return values


def channelize_kernel(rows, x_ref, window_ref, table_ref, out_ref, cos_ref, sin_ref):
    matrix = table_ref[...] * window_ref[...]
    high = matrix.astype(jnp.bfloat16)
    low = (matrix - high.astype(jnp.float32)).astype(jnp.bfloat16)
    both = jnp.concatenate([high, low], axis=1)
    x = x_ref[...]
    y = lax.dot_general(
        jnp.concatenate([x, x], axis=1),
        both,
        (((1,), (1,)), ((), ())),
        preferred_element_type=jnp.float32,
    )
    cos_ref[...] = y[:, :FFT_LEN]
    sin_ref[...] = y[:, FFT_LEN:]
    chunk = lax.broadcasted_iota(jnp.int32, (rows, LANES), 1) // AVG
    tiles = SPEC // CH_OUT
    for tile in range(tiles):
        real, imag = [], []
        for m in range(CH_OUT):
            t = tile * CH_OUT + m
            even = pl.ds(2 * t, rows, stride=2 * SPEC)
            odd = pl.ds(2 * t + 1, rows, stride=2 * SPEC)
            re = cos_ref[even, :] + sin_ref[odd, :]
            im = cos_ref[odd, :] - sin_ref[even, :]
            if m:
                re = pltpu.roll(re, m * AVG, 1)
                im = pltpu.roll(im, m * AVG, 1)
            real.append(re)
            imag.append(im)
        for p, part in enumerate((real, imag)):
            part = barrel([part[-i % CH_OUT] for i in range(CH_OUT)], chunk)
            at = (p * tiles + tile) * LANES
            for k in range(CH_OUT):
                out_ref[k, :, at : at + LANES] = part[k].astype(jnp.bfloat16)


def channelize(block, window):
    rows = block.shape[0]
    flat = block.reshape(rows * SPEC * 2, FFT_LEN)
    return pl.pallas_call(
        functools.partial(channelize_kernel, rows),
        out_shape=jax.ShapeDtypeStruct((CH_OUT, rows, 2 * SPEC * AVG), jnp.bfloat16),
        scratch_shapes=[pltpu.VMEM((rows * SPEC * 2, FFT_LEN), jnp.float32)] * 2,
    )(flat, window[None, :], jnp.asarray(trig_table()))


def correlate_kernel(groups, rows, god_ref, om_ref, x_ref, out_ref, *vis_refs):
    x = x_ref[...]
    half = x.shape[1] // 2
    swapped = jnp.concatenate([x[:, half:], -x[:, :half]], axis=1)
    per_tile = LANES // rows
    per_row = groups // out_ref.shape[0]
    chunk = lax.broadcasted_iota(jnp.int32, (rows // per_tile, LANES), 1) // rows
    for p, left in enumerate((x, swapped)):
        vis = lax.dot_general(
            left, x, (((1,), (1,)), ((), ())), preferred_element_type=jnp.float32
        )
        vis = vis * (1.0 / (AVG * SPEC))
        for h, ref in enumerate(vis_refs):
            ref[p] = vis[:, h * LANES : (h + 1) * LANES]
    for s in range(groups):
        g1 = god_ref[s]
        f, r = g1 // per_row, g1 % per_row
        for h, ref in enumerate(vis_refs):
            owners = [om_ref[g1, god_ref[h * per_tile + c]] for c in range(per_tile)]
            for p in range(2):
                parts = []
                for m in range(per_tile):
                    u = ref[p, pl.ds(s * rows + m, rows // per_tile, stride=per_tile), :]
                    parts.append(pltpu.roll(u, m * rows, 1) if m else u)
                parts = barrel([parts[-i % per_tile] for i in range(per_tile)], chunk)
                for c in range(per_tile):
                    block = parts[c]
                    if c:
                        block = pltpu.roll(block, LANES - c * rows, 1)
                    out_ref[f, owners[c], p, r] = block.astype(jnp.bfloat16)


def correlate(turned, group_of_device, owner_map, bands):
    groups = group_of_device.shape[0]
    rows = turned.shape[0] // groups
    per_tile = LANES // rows
    vmem = pl.BlockSpec(memory_space=pltpu.VMEM)
    smem = pl.BlockSpec(memory_space=pltpu.SMEM)
    return pl.pallas_call(
        functools.partial(correlate_kernel, groups, rows),
        in_specs=[smem, smem, vmem],
        out_specs=vmem,
        out_shape=jax.ShapeDtypeStruct(
            (bands, groups, 2, groups // bands, rows // per_tile, LANES), jnp.bfloat16
        ),
        scratch_shapes=[pltpu.VMEM((2, groups * rows, LANES), jnp.float32)]
        * (groups // per_tile),
    )(group_of_device, owner_map, turned)


def with_swapped(spectra):
    half = spectra.shape[2] // 2
    return jnp.stack(
        [spectra, jnp.concatenate([spectra[..., half:], -spectra[..., :half]], axis=-1)]
    )


def correlate_wide(stacked, remote):
    block = jnp.einsum("pcak,cbk->pcab", stacked, remote, preferred_element_type=jnp.float32)
    return (block * (1.0 / (AVG * SPEC))).astype(jnp.bfloat16)


def wide_plan(local, group_of_device, owner_map, here, groups):
    order = jnp.arange(groups, dtype=jnp.int32)
    device_of_group = jnp.zeros((groups,), jnp.int32).at[group_of_device].set(order)
    rows_in = local.shape[1]
    spread = groups // CH_OUT
    quarter = here % spread
    copies = jnp.repeat(local, spread, axis=0)
    turned = lax.all_to_all(copies, "stn", split_axis=0, concat_axis=1, tiled=True)
    span = CH_OUT * rows_in
    mine = lax.dynamic_slice_in_dim(turned, quarter * span, span, 1)
    block = correlate_wide(with_swapped(mine), turned)
    column_for = (
        jnp.zeros((groups, groups), jnp.int32)
        .at[order[:, None], owner_map]
        .set(jnp.broadcast_to(order[None, :], (groups, groups)))
    )
    row_source = quarter * CH_OUT + jnp.arange(CH_OUT, dtype=jnp.int32)
    row_group = group_of_device[row_source]
    column_device = device_of_group[column_for[row_group]]
    vis = block.reshape(2, CH_OUT, rows_in, groups, rows_in).transpose(0, 1, 3, 2, 4)
    picked = jnp.take_along_axis(vis, column_device[None, :, :, None, None], axis=2)
    outgoing = picked.reshape(2, CH_OUT, groups, rows_in * rows_in)
    received = lax.all_to_all(outgoing, "stn", split_axis=2, concat_axis=2, tiled=True)
    arranged = received.reshape(2, CH_OUT, CH_OUT, spread, rows_in * rows_in).transpose(
        0, 2, 3, 1, 4
    )
    arranged = arranged.reshape(2, CH_OUT, groups, rows_in * rows_in)
    by_group = jnp.take(arranged, device_of_group, axis=2)
    regrouped = lax.all_to_all(by_group, "freq", split_axis=2, concat_axis=1, tiled=True)
    return regrouped[:, :, None]


def shards(samples, window, group_of_device, owner_map):
    groups = lax.axis_size("stn")
    bands = lax.axis_size("freq")
    here = lax.axis_index("stn")
    local = channelize(samples[0], window)
    if groups != CH_OUT:
        return wide_plan(local, group_of_device, owner_map, here, groups)
    rows = local.shape[1]
    turned = lax.all_to_all(local, "stn", split_axis=0, concat_axis=0, tiled=True)
    blocks = correlate(
        turned.reshape(groups * rows, local.shape[2]), group_of_device, owner_map, bands
    )
    shape = blocks.shape
    blocks = blocks.reshape((bands * groups,) + shape[2:])
    owned = lax.all_to_all(blocks, ("freq", "stn"), split_axis=0, concat_axis=0, tiled=True)
    owned = owned.transpose(1, 0, 2, 3, 4)
    return owned.reshape(2, bands * CH_OUT, 1, groups // bands, rows * rows)


def solution(mesh):
    return jax.shard_map(
        shards,
        mesh=mesh,
        in_specs=(P("freq", "stn", None, None, None), P(), P(), P()),
        out_specs=P(None, None, "stn", "freq", None),
        check_vma=False,
    )
```

time: 58.4 us -> 40.6 us (0.70)
  blocking collectives: 8.59 us -> 33.2 us
  local copies, waits for them, and re-layouts: 21.1 us -> 0.95 us
  waiting for transfers between devices: 13.8 us -> 0 us
  starting transfers between devices: 10.9 us -> 0 us
  Pallas kernels: 0 us -> 6.16 us
  matrix products: 2.02 us -> 0 us
  other arithmetic: 1.33 us -> 0 us
    all_to_all x1 -> x2, blocking collectives: 8.59 us -> 33.2 us  [the longest x1 19.4 us: shards(): lax.all_to_all(local, 'stn', split_axis=0, concat_axis=0, tiled=True)]
    all_to_all x2 -> x0, waiting for transfers between devices: 13.8 us -> none  [the longest x1 8.8 us: channel_plan(): lax.all_to_all(outgoing, 'stn', split_axis=2, concat_axis=2, tiled=True)]
    all_to_all x2 -> x0, starting transfers between devices: 10.9 us -> none  [the longest x1 7.28 us: channel_plan(): lax.all_to_all(copies, 'stn', split_axis=0, concat_axis=1, tiled=True)]
    pallas_call x0 -> x2, Pallas kernels: none -> 6.16 us  [the longest x1 3.44 us: correlate(): pl.pallas_call(functools.partial(correlate_kernel, groups, rows), in_spec...]
    gather x10 -> x0, local copies, waits for them, and re-layouts: 4.83 us -> none  [the longest x4 2.13 us: channel_plan(): jnp.take_along_axis(vis, column_device[None, :, :, None, None], axis=2)]
    scatter x2 -> x0, local copies, waits for them, and re-layouts: 4.05 us -> none  [the longest x1 3.45 us: channel_plan(): column_for = jnp.zeros((groups, groups), jnp.int32).at[order[:, None], ow...]
    reshape x3 -> x2, local copies, waits for them, and re-layouts: 4.75 us -> 0.95 us  [shards(): return owned.reshape(2, bands * CH_OUT, 1, groups // bands, rows * rows)]
    transpose x1 -> x0, local copies, waits for them, and re-layouts: 2.86 us -> none  [channelize(): spectra.transpose(3, 0, 2, 1, 4).reshape(CH_OUT, rows, 2 * SPEC * AVG)]
  transfers between devices with their start and end apart: 2 -> 0, of which waited for: 2 -> 0; matrix products, arithmetic and copies ran while one was open for 11% -> 0% of each run, Pallas kernels for 0% -> 0%
where the time goes in v1:
time: 40.6 us; the launch traced here: 40.3 us
  blocking collectives  33.2 us (82%)
  Pallas kernels  6.16 us (15%)
  local copies, waits for them, and re-layouts  0.95 us (2%)
    all_to_all x1, blocking collectives, shards(): lax.all_to_all(local, 'stn', split_axis=0, concat_axis=0, tiled=True)  19.4 us
    all_to_all x1, blocking collectives, shards(): lax.all_to_all(blocks, ('freq', 'stn'), split_axis=0, concat_axis=0, tile...  13.8 us
    pallas_call x1, Pallas kernels, correlate(): pl.pallas_call(functools.partial(correlate_kernel, groups, rows), in_spec...  3.44 us
    pallas_call x1, Pallas kernels, channelize(): pl.pallas_call(functools.partial(channelize_kernel, rows), out_shape=jax....  2.72 us
    reshape x2, local copies, waits for them, and re-layouts, shards(): return owned.reshape(2, bands * CH_OUT, 1, groups // bands, rows * rows)  0.95 us

profile of v1, /device:TPU:0, one launch (start us, length us, event | category | flops | bytes accessed | tf_op | source)
XLA Modules:
  0.0 40.3 jit_solution(9001448093175477069)
XLA Ops:
  0.0 2.7 %shard_map.55 = bf16[8,32,768]{2,1,0:T(8,128)(2,1)} custom-call(bf16[1536,128]{1,0:T(8,128)(2,1)} %bitcast.12, f32[1,128]{1,0:T(1,128)} %bitcast.13, f32[256,128]{1,0:T(8,128)} %constant.2.clone.table_ref), custom_call_target="tpu_custom_call" | custom-call | tf_op jit(solution)/shard_map/pallas_call | solution.py:75
  2.7 19.4 %all_to_all.10 = bf16[8,32,768]{2,1,0:T(8,128)(2,1)} all-to-all(bf16[8,32,768]{2,1,0:T(8,128)(2,1)} %shard_map.55), channel_id=1, replica_groups=mesh['freq'=4,'stn'=8] {'stn'}, dimensions={0} | all-to-all | bytes 786432 | tf_op jit(solution)/shard_map/all_to_all | solution.py:184
  22.2 3.4 %shard_map.56 = bf16[4,8,2,2,8,128]{5,4,3,2,1,0:T(8,128)(2,1)} custom-call(s32[8]{0:T(128)} %god_ref.1, s32[8,8]{1,0:T(8,128)} %om_ref.1, bf16[256,768]{1,0:T(8,128)(2,1)} %bitcast.9), custom_call_target="tpu_custom_call" | custom-call | tf_op jit(solution)/shard_map/pallas_call | solution.py:120
  25.6 13.8 %all_to_all.11 = bf16[32,2,2,8,128]{4,3,2,1,0:T(8,128)(2,1)S(1)} all-to-all(bf16[32,2,2,8,128]{4,3,2,1,0:T(8,128)(2,1)} %bitcast.10), channel_id=1, replica_groups=mesh['freq'=4,'stn'=8] {'freq','stn'}, dimensions={0} | all-to-all | bytes 524288 | tf_op jit(solution)/shard_map/all_to_all | solution.py:190
  39.4 0.1 reshape.12
  39.4 0.9 %copy.7 = bf16[2,32,1,2,1024]{4,3,2,1,0:T(2,128)(2,1)} copy(bf16[2,32,1,2,1024]{4,3,0,1,2:T(2,128)(2,1)S(1)} %reshape.12) | data formatting | bytes 524288 | tf_op jit(solution)/shard_map/reshape | solution.py:192
